TPU v7x, 256 devices: a whole 4x4x8 slice. The times are simulated.
256 devices in a mesh: tm: 128 (over y, z, x), batch: 2 (over core).
Axes of the slice: x: 4, y: 4, z: 8, core: 2. Of those that a mesh axis runs over, the one named last changes fastest.
Arguments:
- gate_in: bfloat16 [8192, 4096], P('tm', 'batch'), parts along dimension 1, may hold values from -4.5 to 8.75
- cand_in: bfloat16 [8192, 4096], P('tm', 'batch'), parts along dimension 1, may hold values from -6 to 6
- rates: float32 [4096], P('batch'), parts along dimension 0, may hold values from 1.2207031e-05 to 0.5
- init_state: float32 [4096], P('batch'), parts along dimension 0, may hold values from -5 to 5
- recur_weight: bfloat16 [2048, 2048], replicated, may hold values from -0.5 to 0.5
Outputs:
- trajectory: float32 [8192, 4096], P('tm', 'batch'), parts along dimension 1
- step_norms: float32 [6], P('batch'), parts along dimension 0
There are 2 independent parts, one for each index of `batch`. A program takes and returns all parts, laid end to end along the dimension named above; an argument that names none is the same for every part. Nothing has to cross between parts.
All inputs are finite; a program needn't handle non-finite values.
Results may differ from a plain program's by a relative error of at most 0.0012.
Values sent between devices are 32-bit elements; how exact they have to be, the bound alone decides.
A program may use at most 64 MiB of HBM per device.

v0:
```python
import functools

import jax
import jax.numpy as jnp
from jax import lax
from jax.sharding import Mesh
from jax.sharding import PartitionSpec as P

ITERS = 3
TM = ("tm_0", "tm_1", "tm_2")


def nothing_yet(x, identity):
    return jax.tree.map(
        lambda a, e: jnp.broadcast_to(jnp.asarray(e, a.dtype), a.shape), x, identity
    )


def collected_together(x, axis):
    leaves = jax.tree.leaves(x)
    sequence = sorted(range(len(leaves)), key=lambda k: -leaves[k].size)
    width = (1, *leaves[sequence[0]].shape)[-1]
    lines = [
        jnp.pad(leaves[k].reshape(-1), (0, -leaves[k].size % width)).reshape(-1, width)
        for k in sequence
    ]
    both, at, found = (lax.all_gather(jnp.concatenate(lines), axis), 0, {})
    for k, line in zip(sequence, lines):
        section = both[:, at : at + len(line)].reshape(len(both), -1)
        found[k] = section[:, : leaves[k].size].reshape(-1, *leaves[k].shape)
        at += len(line)
    numbers = iter(range(len(leaves)))
    return jax.tree.map(lambda _: found[next(numbers)], x)


def gathered_by_type(x, axis):
    leaves, found = (jax.tree.leaves(x), {})
    for first, a in enumerate(leaves):
        if first not in found:
            alike = [k for k, b in enumerate(leaves) if b.dtype == a.dtype]
            got = (
                collected_together([leaves[k] for k in alike], axis)
                if len(alike) > 1
                else [lax.all_gather(a, axis)]
            )
            for k, b in zip(alike, got):
                found[k] = b
    numbers = iter(range(len(leaves)))
    return jax.tree.map(lambda _: found[next(numbers)], x)


def prefix_by_axis(x, axes, combine, identity):
    before = start = nothing_yet(x, identity)
    so_far = x
    for axis in reversed(axes):
        peers, place = (lax.axis_size(axis), lax.axis_index(axis))
        pieces = gathered_by_type(so_far, axis)
        inside, so_far = (start, start)
        for k in range(peers):
            passed = k < place
            so_far = combine(so_far, jax.tree.map(lambda part: part[k], pieces))
            inside = jax.tree.map(lambda new, old: jnp.where(passed, new, old), so_far, inside)
        before = combine(inside, before)
    return before


def over_axes(x, axes):
    return functools.reduce(lax.psum, axes, x)


def link(earlier, later):
    return (later[0] * earlier[0], later[0] * earlier[1] + later[1])


def body(gate_in, cand_in, rates, init_state, recur_weight):
    rows, width = gate_in.shape
    devices = lax.axis_size(TM)
    first = lax.axis_index(TM) == 0
    gate = gate_in.astype(jnp.float32)
    keep = jnp.exp(-rates[None, :] * jax.nn.softplus(gate) - jnp.maximum(gate - 8.0, 0.0))
    cand_base = cand_in.astype(jnp.float32)
    unit_diag = jnp.diagonal(recur_weight).astype(jnp.float32)
    state = jnp.zeros((rows, width), jnp.float32)
    entry = jnp.where(first, init_state, jnp.zeros_like(init_state))
    ones = jnp.ones((width,), jnp.float32)
    zeros = jnp.zeros((width,), jnp.float32)
    totals = []
    for step in range(ITERS):
        before = entry
        prev = jnp.concatenate([before[None, :], state[: rows - 1]], axis=0)
        mixed = jnp.dot(prev.astype(jnp.bfloat16), recur_weight, preferred_element_type=jnp.float32)
        cand = jnp.tanh(cand_base + mixed)
        mapped = keep * prev + (1.0 - keep) * cand
        slope = keep + (1.0 - keep) * (1.0 - cand * cand) * unit_diag[None, :]
        offset = mapped - slope * prev
        cum_a, cum_b = lax.associative_scan(link, (slope, offset), axis=0)
        reach_a, reach_b = prefix_by_axis(
            (cum_a[rows - 1], cum_b[rows - 1]), TM, link, (ones, zeros)
        )
        entry = reach_a * init_state + reach_b
        fresh = cum_b + cum_a * entry[None, :]
        delta = fresh - state
        local = jnp.sum(delta * delta)
        totals.append(local)
        state = fresh
    summed = over_axes(jnp.stack(totals), TM)
    return (state, jnp.sqrt(summed / (rows * devices * width)))


def solution(mesh):
    torus = Mesh(
        mesh.devices.reshape(4, 8, 4, mesh.shape["batch"]), ("tm_0", "tm_1", "tm_2", "batch")
    )
    placed = (P(TM, "batch"), P(TM, "batch"), P("batch"), P("batch"), P())
    return jax.shard_map(
        body, mesh=torus, in_specs=placed, out_specs=(P(TM, "batch"), P("batch")), check_vma=False
    )
```

profile of v0, /device:TPU:8, one launch (start us, length us, event | category | flops | bytes accessed | tf_op | source)
XLA Modules:
  0.0 253.8 jit_solution(3822778831365155377)
XLA Ops:
  0.7 0.7 neg.8
  1.4 32.0 %gather_fusion = bf16[2048]{0:T(1024)(128)(2,1)S(1)} fusion(bf16[2048,2048]{1,0:T(8,128)(2,1)} %param.9, s32[2048]{0:T(1024)S(1)} %bitcast.510), kind=kCustom, calls=%fused_computation | custom fusion | bytes 24576 | tf_op jit(solution)/shard_map/jit(diagonal)/cond/branch_0_fun/gather | solution.py:82
  33.5 5.5 %multiply_add_fusion.5 = (f32[64,2048]{1,0:T(8,128)S(1)}, f32[64,2048]{1,0:T(8,128)S(1)}) fusion(f32[2048]{0:T(1024)S(1)} %convert_element_type.25, bf16[64,2048]{1,0:T(8,128)(2,1)} %param.5, f32[2048]{0:T(1024)S(1)} %neg.8, f32[1,2048]{1,0:T(1,128)S(1)} %bitcast.515, bf16[2048,2048]{1,0:T(8,128)(2,1)} %param.9, bf16[64,2048]{1,0:T(8,128)(2,1)} %param.6), kind=kOutput, calls=%fused_computation.36 | convolution fusion | flops 540016640 | bytes 9986048 | tf_op jit(solution)/shard_map/dot_general | solution.py:91
  39.0 0.1 slice.1036
  39.2 0.1 slice.1035
  39.3 0.2 slice.1034
  39.6 0.2 slice.1087
  39.8 0.1 slice.1063
  39.9 0.1 slice.1062
  42.4 0.1 add_multiply_fusion.5
  42.6 0.1 pad.245
  42.7 0.1 pad.233
  42.8 0.1 pad.234
  42.9 0.1 pad.246
  43.0 12.2 %all-gather.9 = f32[4,2,2048]{2,1,0:T(2,128)S(1)} all-gather(f32[1,2,2048]{2,1,0:T(2,128)S(1)} %maximum_bitcast_fusion), channel_id=2, replica_groups=mesh['tm_0'=4,'tm_1'=8,'tm_2'=4,'batch'=2] {'tm_2'}, dimensions={0}, use_global_device_ids=true | all-gather | bytes 81920 | tf_op jit(solution)/shard_map/all_gather | solution.py:27
  55.4 28.2 %all-gather.10 = f32[8,2,2048]{2,1,0:T(2,128)S(1)} all-gather(f32[1,2,2048]{2,1,0:T(2,128)S(1)} %maximum_bitcast_fusion.1), channel_id=3, replica_groups=mesh['tm_0'=4,'tm_1'=8,'tm_2'=4,'batch'=2] {'tm_1'}, dimensions={0}, use_global_device_ids=true | all-gather | bytes 147456 | tf_op jit(solution)/shard_map/all_gather | solution.py:27
  83.6 0.1 bitcast_add_fusion.24
  83.7 0.1 fusion.102
  83.8 12.1 %all-gather.11 = f32[4,2,2048]{2,1,0:T(2,128)S(1)} all-gather(f32[1,2,2048]{2,1,0:T(2,128)S(1)} %maximum_bitcast_fusion.2), channel_id=4, replica_groups=mesh['tm_0'=4,'tm_1'=8,'tm_2'=4,'batch'=2] {'tm_0'}, dimensions={0}, use_global_device_ids=true | all-gather | bytes 81920 | tf_op jit(solution)/shard_map/all_gather | solution.py:27
  96.0 0.1 add_add_fusion.2
  96.0 0.1 multiply_add_fusion.4
  96.2 5.5 %multiply_add_fusion.3 = (f32[64,2048]{1,0:T(8,128)S(1)}, f32[64,2048]{1,0:T(8,128)S(1)}) fusion(f32[2048]{0:T(1024)S(1)} %convert_element_type.25, bf16[64,2048]{1,0:T(8,128)(2,1)S(1)} %copy-done, f32[2048]{0:T(1024)S(1)} %neg.8, f32[63,2048]{1,0:T(8,128)S(1)} %bitcast.511, f32[1,2048]{1,0:T(1,128)S(1)} %bitcast.514, bf16[2048,2048]{1,0:T(8,128)(2,1)} %param.9, ...), kind=kOutput, calls=%fused_computation.34 | convolution fusion | flops 540672000 | bytes 10502144 | tf_op jit(solution)/shard_map/dot_general | solution.py:91
  101.7 0.1 slice.1125
  101.9 0.1 slice.1124
  102.0 0.2 slice.1123
  102.2 0.2 slice.1176
  102.4 0.1 slice.1152
  102.6 0.1 slice.1151
  105.0 0.1 add_multiply_fusion.3
  105.3 0.1 pad.269
  105.4 0.1 pad.257
  105.4 0.1 pad.258
  105.5 0.1 pad.270
  105.7 11.9 %all-gather.12 = f32[4,2,2048]{2,1,0:T(2,128)S(1)} all-gather(f32[1,2,2048]{2,1,0:T(2,128)S(1)} %maximum_bitcast_fusion.3), channel_id=5, replica_groups=mesh['tm_0'=4,'tm_1'=8,'tm_2'=4,'batch'=2] {'tm_2'}, dimensions={0}, use_global_device_ids=true | all-gather | bytes 81920 | tf_op jit(solution)/shard_map/all_gather | solution.py:27
  117.7 24.8 %all-gather.13 = f32[8,2,2048]{2,1,0:T(2,128)S(1)} all-gather(f32[1,2,2048]{2,1,0:T(2,128)S(1)} %maximum_bitcast_fusion.4), channel_id=6, replica_groups=mesh['tm_0'=4,'tm_1'=8,'tm_2'=4,'batch'=2] {'tm_1'}, dimensions={0}, use_global_device_ids=true | all-gather | bytes 147456 | tf_op jit(solution)/shard_map/all_gather | solution.py:27
  142.4 0.1 bitcast_add_fusion.12
  142.6 0.1 fusion.100
  142.7 11.9 %all-gather.14 = f32[4,2,2048]{2,1,0:T(2,128)S(1)} all-gather(f32[1,2,2048]{2,1,0:T(2,128)S(1)} %maximum_bitcast_fusion.5), channel_id=7, replica_groups=mesh['tm_0'=4,'tm_1'=8,'tm_2'=4,'batch'=2] {'tm_0'}, dimensions={0}, use_global_device_ids=true | all-gather | bytes 81920 | tf_op jit(solution)/shard_map/all_gather | solution.py:27
  154.6 0.1 add_add_fusion.1
  154.7 1.2 multiply_add_fusion.2
  155.8 5.5 %multiply_add_fusion.1 = (f32[64,2048]{1,0:T(8,128)S(1)}, f32[64,2048]{1,0:T(8,128)S(1)}) fusion(f32[2048]{0:T(1024)S(1)} %convert_element_type.25, bf16[64,2048]{1,0:T(8,128)(2,1)S(1)} %copy-done, f32[2048]{0:T(1024)S(1)} %neg.8, f32[63,2048]{1,0:T(8,128)S(1)} %bitcast.512, f32[1,2048]{1,0:T(1,128)S(1)} %bitcast.513, bf16[2048,2048]{1,0:T(8,128)(2,1)} %param.9, ...), kind=kOutput, calls=%fused_computation.31 | convolution fusion | flops 540672000 | bytes 10502144 | tf_op jit(solution)/shard_map/dot_general | solution.py:91
  161.4 0.1 slice.1217
  161.5 0.1 slice.1213
  161.7 0.2 slice.1212
  161.9 0.8 slice.1253
  162.7 0.1 slice.1215
  162.9 0.1 slice.1214
  165.3 0.1 add_multiply_fusion
  165.6 0.1 pad.281
  165.6 0.1 pad.293
  165.7 0.1 pad.294
  165.8 0.1 pad.282
  165.9 11.9 %all-gather.15 = f32[4,2,2048]{2,1,0:T(2,128)S(1)} all-gather(f32[1,2,2048]{2,1,0:T(2,128)S(1)} %maximum_bitcast_fusion.6), channel_id=8, replica_groups=mesh['tm_0'=4,'tm_1'=8,'tm_2'=4,'batch'=2] {'tm_2'}, dimensions={0}, use_global_device_ids=true | all-gather | bytes 81920 | tf_op jit(solution)/shard_map/all_gather | solution.py:27
  177.9 24.6 %all-gather.16 = f32[8,2,2048]{2,1,0:T(2,128)S(1)} all-gather(f32[1,2,2048]{2,1,0:T(2,128)S(1)} %maximum_bitcast_fusion.7), channel_id=9, replica_groups=mesh['tm_0'=4,'tm_1'=8,'tm_2'=4,'batch'=2] {'tm_1'}, dimensions={0}, use_global_device_ids=true | all-gather | bytes 147456 | tf_op jit(solution)/shard_map/all_gather | solution.py:27
  202.5 0.1 bitcast_add_fusion
  202.7 0.1 fusion.98
  202.8 11.8 %all-gather.17 = f32[4,2,2048]{2,1,0:T(2,128)S(1)} all-gather(f32[1,2,2048]{2,1,0:T(2,128)S(1)} %maximum_bitcast_fusion.8), channel_id=10, replica_groups=mesh['tm_0'=4,'tm_1'=8,'tm_2'=4,'batch'=2] {'tm_0'}, dimensions={0}, use_global_device_ids=true | all-gather | bytes 81920 | tf_op jit(solution)/shard_map/all_gather | solution.py:27
  214.7 0.1 add_add_fusion
  214.8 1.7 multiply_reduce_fusion.2
  216.4 1.9 pad_maximum_fusion.32
  218.3 8.4 %psum.21 = f32[3]{0:T(128)S(1)} all-reduce(f32[3]{0:T(128)S(1)} %pad_maximum_fusion.32), channel_id=1, replica_groups=mesh['tm_0'=4,'tm_1'=8,'tm_2'=4,'batch'=2] {'tm_0'}, use_global_device_ids=true, to_apply=%region_3.4 | all-reduce | flops 3 | bytes 24 | tf_op jit(solution)/shard_map/psum | solution.py:68
  226.8 16.4 %psum.22 = f32[3]{0:T(128)S(1)} all-reduce(f32[3]{0:T(128)S(1)} %psum.21), channel_id=1, replica_groups=mesh['tm_0'=4,'tm_1'=8,'tm_2'=4,'batch'=2] {'tm_1'}, use_global_device_ids=true, to_apply=%region_4.5 | all-reduce | flops 3 | bytes 24 | tf_op jit(solution)/shard_map/psum | solution.py:68
  243.1 10.1 %psum.23 = f32[3]{0:T(128)S(1)} all-reduce(f32[3]{0:T(128)S(1)} %psum.22), channel_id=1, replica_groups=mesh['tm_0'=4,'tm_1'=8,'tm_2'=4,'batch'=2] {'tm_2'}, use_global_device_ids=true, to_apply=%region_5.6 | all-reduce | flops 3 | bytes 24 | tf_op jit(solution)/shard_map/psum | solution.py:68
  253.3 0.5 multiply_sqrt_fusion
  (266 shorter events, 6.8 us)
Async XLA Ops:
  41.2 54.7 %copy-start.4 = (f32[2048]{0:T(1024)S(1)}, f32[2048]{0:T(1024)}, u32[]{:S(2)}) copy-start(f32[2048]{0:T(1024)} %param.8) | copy-start | bytes 24580
  41.9 54.2 %copy-start = (bf16[64,2048]{1,0:T(8,128)(2,1)S(1)}, bf16[64,2048]{1,0:T(8,128)(2,1)}, u32[]{:S(2)}) copy-start(bf16[64,2048]{1,0:T(8,128)(2,1)} %param.5) | copy-start | bytes 786436
  42.0 54.2 %copy-start.1 = (bf16[64,2048]{1,0:T(8,128)(2,1)S(1)}, bf16[64,2048]{1,0:T(8,128)(2,1)}, u32[]{:S(2)}) copy-start(bf16[64,2048]{1,0:T(8,128)(2,1)} %param.6) | copy-start | bytes 786436
  105.6 49.0 %copy-start.2 = (f32[64,2048]{1,0:T(8,128)}, f32[64,2048]{1,0:T(8,128)S(1)}, u32[]{:S(2)}) copy-start(f32[64,2048]{1,0:T(8,128)S(1)} %pad.270) | copy-start | bytes 1572868
  163.1 2.2 copy-start.3
where the time goes:
time: 255 us; the launch traced here: 254 us
  blocking collectives  184 us (72%)
  local copies, waits for them, and re-layouts  40.9 us (16%)
  matrix products  16.5 us (6%)
  other arithmetic  9.48 us (4%)
  between operations  2.68 us (1%)
    all_gather x9, blocking collectives, collected_together(): both, at, found = (lax.all_gather(jnp.concatenate(lines), axis), 0, {})  149 us
    psum x3, blocking collectives, over_axes(): return functools.reduce(lax.psum, axes, x)  34.9 us
    gather x1, local copies, waits for them, and re-layouts, body(): unit_diag = jnp.diagonal(recur_weight).astype(jnp.float32)  32 us
    dot_general x3, matrix products, body(): jnp.dot(prev.astype(jnp.bfloat16), recur_weight, preferred_element_type=j...  16.5 us
    slice x108, local copies, waits for them, and re-layouts, body(): cum_a, cum_b = lax.associative_scan(link, (slope, offset), axis=0)  6.08 us

commit v1 on v0

v1 whole, which is shorter than its diff:
```python
import functools

import jax
import jax.numpy as jnp
from jax import lax
from jax.experimental import pallas as pl
from jax.experimental.pallas import tpu as pltpu
from jax.sharding import PartitionSpec as P

ITERS = 3
LANES = 128
ROWS = 64
BLOCKS = 8
STEPS = 8
MEMBERS = 8
MESH = pl.DeviceIdType.MESH


def joined(first, second):
    return second[0] * first[0], second[0] * first[1] + second[1]


def kernel(
    groups, tiles, scale,
    gate_hbm, cand_hbm, rates_hbm, init_hbm, weight_hbm,
    out_hbm, norms_ref,
    gate_v, cand_v, weight_v, rates_v, init_v,
    spread, keep_v, base_v, state_v, a_v, b_v, before_a, before_b, whole_a, whole_b,
    diag_v, entry_v, delta_v, low_v, first_low, mixed_v,
    sent1, got1, sent2, got2, start_v, sent3, got3, final_v,
    load_sem, weight_sem, send1, recv1, send2, recv2, send3, recv3, out_sem,
):
    f32 = jnp.float32
    place = lax.axis_index("tm")
    part = lax.axis_index("batch")
    group, member = place // MEMBERS, lax.rem(place, MEMBERS)
    devices = groups * MEMBERS
    width = tiles * LANES
    depth = width // 8

    def at(index):
        return (index, part)

    barrier = pltpu.get_barrier_semaphore()
    for d in range(1, MEMBERS):
        other = group * MEMBERS + lax.rem(member + d, MEMBERS)
        pl.semaphore_signal(barrier, inc=1, device_id=at(other), device_id_type=MESH)
    for d in range(1, groups):
        other = lax.rem(group + d, groups) * MEMBERS + member
        pl.semaphore_signal(barrier, inc=1, device_id=at(other), device_id_type=MESH)

    loads = [
        pltpu.make_async_copy(gate_hbm, gate_v, load_sem.at[0]),
        pltpu.make_async_copy(cand_hbm, cand_v, load_sem.at[1]),
        pltpu.make_async_copy(rates_hbm, rates_v, load_sem.at[2]),
        pltpu.make_async_copy(init_hbm, init_v, load_sem.at[3]),
    ]
    for copy in loads:
        copy.start()
    weight_copies = [
        pltpu.make_async_copy(
            weight_hbm.at[pl.ds(i * depth, depth)], weight_v.at[pl.ds(i * depth, depth)], weight_sem.at[i]
        )
        for i in range(8)
    ]
    for copy in weight_copies:
        copy.start()
    for copy in loads:
        copy.wait()

    block = lax.broadcasted_iota(jnp.int32, (BLOCKS, LANES), 0)
    entry_v[...] = jnp.where(place == 0, init_v[...], 0.0)

    for l in range(tiles):
        cols = pl.ds(l * LANES, LANES)
        spread[0, l] = gate_v[:, cols].astype(f32)
        spread[1, l] = cand_v[:, cols].astype(f32)
        rate = rates_v[pl.ds(l, 1), :]
        for j in range(STEPS):
            rows = pl.ds(j * BLOCKS, BLOCKS)
            gate = spread[0, l, pl.ds(j, BLOCKS, stride=STEPS), :]
            soft = jnp.maximum(gate, 0.0) + jnp.log1p(jnp.exp(-jnp.abs(gate)))
            keep_v[l, rows, :] = jnp.exp(-rate * soft - jnp.maximum(gate - 8.0, 0.0))
            base_v[l, rows, :] = spread[1, l, pl.ds(j, BLOCKS, stride=STEPS), :]

    top = lax.broadcasted_iota(jnp.int32, (16, LANES), 0) == 0
    for l in range(tiles):
        row = jnp.broadcast_to(entry_v[pl.ds(l, 1), :], (16, LANES))
        first_low[:, pl.ds(l * LANES, LANES)] = jnp.where(top, row, 0.0).astype(jnp.bfloat16)
    eye = lax.broadcasted_iota(jnp.int32, (LANES, LANES), 0) == lax.broadcasted_iota(
        jnp.int32, (LANES, LANES), 1
    )
    total = jnp.zeros((16, width), f32)
    for i, copy in enumerate(weight_copies):
        copy.wait()
        for l in range(i * tiles // 8, (i + 1) * tiles // 8):
            corner = weight_v[pl.ds(l * LANES, LANES), pl.ds(l * LANES, LANES)].astype(f32)
            diag_v[pl.ds(l, 1), :] = jnp.sum(jnp.where(eye, corner, 0.0), axis=0, keepdims=True)
        deep = pl.ds(i * depth, depth)
        total = total + jnp.dot(first_low[:, deep], weight_v[deep, :], preferred_element_type=f32)
    mixed_v[pl.ds(0, 16), :] = total

    def local_scan(k, l):
        cols = pl.ds(l * LANES, LANES)
        unit = diag_v[pl.ds(l, 1), :]
        a = b = old = None
        for j in range(STEPS):
            rows = pl.ds(j * BLOCKS, BLOCKS)
            keep = keep_v[l, rows, :]
            arg = base_v[l, rows, :]
            if k > 0 or j == 0:
                arg = arg + mixed_v[rows, cols]
            cand = jnp.tanh(arg)
            rest = 1.0 - keep
            slope = keep + rest * (1.0 - cand * cand) * unit
            step = rest * cand
            if j == 0:
                prev = jnp.broadcast_to(entry_v[pl.ds(l, 1), :], (BLOCKS, LANES))
                last = 0.0 if k == 0 else pltpu.roll(state_v[l, pl.ds(7 * BLOCKS, BLOCKS), :], 1, 0)
                prev = jnp.where(block == 0, prev, last)
                step = step + keep * prev
            elif k > 0:
                step = step + keep * old
            if k > 0:
                old = state_v[l, rows, :]
                step = step - old
            if j == 0:
                a, b = slope, step
            else:
                a, b = slope * a, slope * b + step
            a_v[l, rows, :] = a
            b_v[l, rows, :] = b
        for shift in (1, 2, 4):
            inside = block >= shift
            pa, pb = pltpu.roll(a, shift, 0), pltpu.roll(b, shift, 0)
            b = jnp.where(inside, a * pb + b, b)
            a = jnp.where(inside, a * pa, a)
        whole_a[pl.ds(l * BLOCKS, BLOCKS), :] = a
        whole_b[pl.ds(l * BLOCKS, BLOCKS), :] = b
        before_a[l] = jnp.where(block == 0, 1.0, pltpu.roll(a, 1, 0))
        before_b[l] = jnp.where(block == 0, 0.0, pltpu.roll(b, 1, 0))

    half = tiles // 2

    def exchange(k):
        for i in range(2):
            pick = pl.ds(i * half * BLOCKS + BLOCKS - 1, half, stride=BLOCKS)
            for first, source in ((0, whole_a), (tiles, whole_b)):
                value = source[pick, :]
                sent1[k, pl.ds(first + i * half, half), :] = value
                got1[k, member, pl.ds(first + i * half, half), :] = value
        if k == 0:
            pl.semaphore_wait(barrier, MEMBERS - 1 + groups - 1)
        for d in range(1, MEMBERS):
            other = group * MEMBERS + lax.rem(member + d, MEMBERS)
            pltpu.make_async_remote_copy(
                sent1.at[k], got1.at[k, member], send1.at[k], recv1.at[k],
                device_id=at(other), device_id_type=MESH,
            ).start()
        most = got1.at[k, pl.ds(0, MEMBERS - 1)]
        pltpu.make_async_copy(most, most, recv1.at[k]).wait()

        part_a, part_b = pl.ds(0, tiles), pl.ds(tiles, tiles)
        run = got1[k, 0, part_a, :], got1[k, 0, part_b, :]
        mine = jnp.ones((tiles, LANES), f32), jnp.zeros((tiles, LANES), f32)
        for m in range(1, MEMBERS):
            mine = tuple(jnp.where(member == m, new, old) for new, old in zip(run, mine))
            run = joined(run, (got1[k, m, part_a, :], got1[k, m, part_b, :]))
        sent2[k, part_a, :] = run[0]
        sent2[k, part_b, :] = run[1]
        for d in range(groups - 1, 0, -1):
            @pl.when(group + d < groups)
            def _():
                pltpu.make_async_remote_copy(
                    sent2.at[k], got2.at[k, group], send2.at[k, d], recv2.at[k, group],
                    device_id=at((group + d) * MEMBERS + member), device_id_type=MESH,
                ).start()
        start_v[...] = jnp.zeros((tiles, LANES), f32)
        for q in range(groups - 1):
            @pl.when(q < group)
            def _():
                slot = got2.at[k, q]
                pltpu.make_async_copy(slot, slot, recv2.at[k, q]).wait()
                start_v[...] = got2[k, q, part_a, :] * start_v[...] + got2[k, q, part_b, :]
        delta = mine[0] * start_v[...] + mine[1]
        delta_v[...] = delta
        entry_v[...] = entry_v[...] + delta

    def advance(k, l):
        cols = pl.ds(l * LANES, LANES)
        carry = before_b[l] + before_a[l] * delta_v[pl.ds(l, 1), :]
        change = jnp.zeros((BLOCKS, LANES), f32)
        states = []
        for j in range(STEPS):
            rows = pl.ds(j * BLOCKS, BLOCKS)
            moved = b_v[l, rows, :] + a_v[l, rows, :] * carry
            change = change + moved * moved
            new = moved if k == 0 else state_v[l, rows, :] + moved
            states.append(new)
            if k < ITERS - 1:
                state_v[l, rows, :] = new
            else:
                spread[0, l, pl.ds(j, BLOCKS, stride=STEPS), :] = new
        if k < ITERS - 1:
            head = jnp.broadcast_to(entry_v[pl.ds(l, 1), :], (BLOCKS, LANES))
            prevs = [jnp.where(block == 0, head, pltpu.roll(states[-1], 1, 0))] + states[:-1]
            for i in range(STEPS // 2):
                pair = jnp.concatenate(prevs[2 * i : 2 * i + 2], axis=0)
                low_v[pl.ds(i * 16, 16), cols] = pair.astype(jnp.bfloat16)
        else:
            pltpu.make_async_copy(spread.at[0, l], out_hbm.at[:, cols], out_sem.at[l]).start()
        return change

    lane = lax.broadcasted_iota(jnp.int32, (1, LANES), 1)
    totals = jnp.zeros((1, LANES), f32)
    for l in range(tiles):
        local_scan(0, l)
    for k in range(ITERS):
        exchange(k)
        change = jnp.zeros((BLOCKS, LANES), f32)
        for l in range(tiles):
            change = change + advance(k, l)
        totals = jnp.where(lane == k, jnp.sum(change), totals)
        if k < ITERS - 1:
            wide = 512
            for n in range(width // wide):
                cols = pl.ds(n * wide, wide)
                mixed_v[:, cols] = jnp.dot(low_v[...], weight_v[:, cols], preferred_element_type=f32)
                for l in range(n * wide // LANES, (n + 1) * wide // LANES):
                    local_scan(k + 1, l)

    sent3[...] = totals
    got3[place] = totals

    def send_total(d, carry):
        pltpu.make_async_remote_copy(
            sent3, got3.at[place], send3, recv3,
            device_id=at(lax.rem(place + d, devices)), device_id_type=MESH,
        ).start()
        return carry

    lax.fori_loop(1, devices, send_total, 0)
    most = got3.at[pl.ds(0, devices - 1)]
    for l in range(tiles):
        pltpu.make_async_copy(spread.at[0, l], out_hbm.at[:, pl.ds(l * LANES, LANES)], out_sem.at[l]).wait()
    for k in range(ITERS):
        sent = got1.at[k, pl.ds(0, MEMBERS - 1)]
        pltpu.make_async_copy(sent, sent, send1.at[k]).wait()
        for d in range(1, groups):
            @pl.when(group + d < groups)
            def _():
                pltpu.make_async_copy(sent2.at[k], sent2.at[k], send2.at[k, d]).wait()
    pltpu.make_async_copy(most, most, recv3).wait()
    pltpu.make_async_copy(most, most, send3).wait()
    norms_ref[...] = jnp.sqrt(jnp.sum(got3[...], axis=0) * scale)


def body(gate_in, cand_in, rates, init_state, recur_weight):
    rows, width = gate_in.shape
    devices = lax.axis_size("tm")
    groups, tiles = devices // MEMBERS, width // LANES
    f32, bf16 = jnp.float32, jnp.bfloat16
    hbm = pl.BlockSpec(memory_space=pltpu.HBM)
    dma = pltpu.SemaphoreType.DMA
    panel = pltpu.VMEM((tiles, rows, LANES), f32)
    edge = pltpu.VMEM((tiles, BLOCKS, LANES), f32)
    ends = pltpu.VMEM((tiles * BLOCKS, LANES), f32)
    units = pltpu.VMEM((tiles, LANES), f32)
    out, norms = pl.pallas_call(
        functools.partial(kernel, groups, tiles, 1.0 / (rows * devices * width)),
        out_shape=(
            jax.ShapeDtypeStruct((rows, width), f32),
            jax.ShapeDtypeStruct((1, LANES), f32),
        ),
        in_specs=[hbm] * 5,
        out_specs=(hbm, pl.BlockSpec(memory_space=pltpu.VMEM)),
        scratch_shapes=[
            pltpu.VMEM((rows, width), bf16),
            pltpu.VMEM((rows, width), bf16),
            pltpu.VMEM((width, width), bf16),
            units, units,
            pltpu.VMEM((2, tiles, rows, LANES), f32),
            panel, panel, panel, panel, panel, edge, edge, ends, ends,
            units, units, units,
            pltpu.VMEM((rows, width), bf16),
            pltpu.VMEM((16, width), bf16),
            pltpu.VMEM((rows, width), f32),
            pltpu.VMEM((ITERS, 2 * tiles, LANES), f32),
            pltpu.VMEM((ITERS, MEMBERS, 2 * tiles, LANES), f32),
            pltpu.VMEM((ITERS, 2 * tiles, LANES), f32),
            pltpu.VMEM((ITERS, groups, 2 * tiles, LANES), f32),
            units,
            pltpu.VMEM((1, LANES), f32),
            pltpu.VMEM((devices, 1, LANES), f32),
            pltpu.VMEM((8, LANES), f32),
            dma((4,)), dma((8,)),
            dma((ITERS,)), dma((ITERS,)),
            dma((ITERS, groups)), dma((ITERS, groups)),
            dma, dma, dma((tiles,)),
        ],
        compiler_params=pltpu.CompilerParams(collective_id=0, has_side_effects=True),
        name="newton",
    )(gate_in, cand_in, rates.reshape(tiles, LANES), init_state.reshape(tiles, LANES), recur_weight)
    return out, norms[0, :ITERS]


def solution(mesh):
    placed = (P("tm", "batch"), P("tm", "batch"), P("batch"), P("batch"), P())
    return jax.shard_map(
        body, mesh=mesh, in_specs=placed, out_specs=(P("tm", "batch"), P("batch")), check_vma=False
    )
```

time: 255 us -> 65.1 us (0.26)
  blocking collectives: 184 us -> 0 us
  Pallas kernels: 0 us -> 61.1 us
  local copies, waits for them, and re-layouts: 40.9 us -> 2.98 us
  matrix products: 16.5 us -> 0 us
  other arithmetic: 9.48 us -> 0 us
    all_gather x9 -> x0, blocking collectives: 149 us -> none  [collected_together(): both, at, found = (lax.all_gather(jnp.concatenate(lines), axis), 0, {})]
    pallas_call x0 -> x1, Pallas kernels: none -> 61.1 us  [body(): pl.pallas_call(functools.partial(kernel, groups, tiles, 1.0 / (rows * dev...]
    psum x3 -> x0, blocking collectives: 34.9 us -> none  [over_axes(): return functools.reduce(lax.psum, axes, x)]
    gather x1 -> x0, local copies, waits for them, and re-layouts: 32 us -> none  [body(): unit_diag = jnp.diagonal(recur_weight).astype(jnp.float32)]
    dot_general x3 -> x0, matrix products: 16.5 us -> none  [body(): jnp.dot(prev.astype(jnp.bfloat16), recur_weight, preferred_element_type=j...]
    slice x117 -> x0, local copies, waits for them, and re-layouts: 6.68 us -> none  [the longest x108 6.08 us: body(): cum_a, cum_b = lax.associative_scan(link, (slope, offset), axis=0)]
where the time goes in v1:
time: 65.1 us; the launch traced here: 64.7 us
  Pallas kernels  61.1 us (94%)
  local copies, waits for them, and re-layouts  2.98 us (5%)
    pallas_call x1, Pallas kernels, body(): pl.pallas_call(functools.partial(kernel, groups, tiles, 1.0 / (rows * dev...  61.1 us
    unnamed x1, local copies, waits for them, and re-layouts  1.87 us

profile of v1, /device:TPU:8, one launch (start us, length us, event | category | flops | bytes accessed | tf_op | source)
XLA Modules:
  0.0 64.7 jit_solution(14077183007147302186)
XLA Ops:
  0.6 61.1 %newton.1 = (f32[64,2048]{1,0:T(8,128)}, f32[1,128]{1,0:T(1,128)}) custom-call(bf16[64,2048]{1,0:T(8,128)(2,1)} %gate_hbm.1, bf16[64,2048]{1,0:T(8,128)(2,1)} %cand_hbm.1, f32[16,128]{1,0:T(8,128)} %bitcast.4, f32[16,128]{1,0:T(8,128)} %bitcast.5, bf16[2048,2048]{1,0:T(8,128)(2,1)} %weight_hbm.1), custom_call_target="tpu_custom_call" | custom-call | tf_op jit(solution)/shard_map/newton/pallas_call | solution.py:269
  61.7 1.1 %slice_bitcast_fusion = f32[3]{0:T(128)} fusion(f32[1,128]{1,0:T(1,128)} %get-tuple-element.5), kind=kLoop, calls=%fused_computation | loop fusion | bytes 24 | tf_op jit(solution)/shard_map/squeeze | solution.py:304
  62.8 1.9 %copy.8 = f32[64,2048]{1,0:T(8,128)} copy(f32[64,2048]{1,0:T(8,128)} %get-tuple-element.8) | data formatting | bytes 1048576

commit v2 on v1

--- a/solution.py
+++ b/solution.py
@@ -13,6 +13,7 @@
 BLOCKS = 8
 STEPS = 8
 MEMBERS = 8
+NY, NZ, NX = 4, 8, 4
 MESH = pl.DeviceIdType.MESH
 
 
@@ -23,12 +24,12 @@
 def kernel(
     groups, tiles, scale,
     gate_hbm, cand_hbm, rates_hbm, init_hbm, weight_hbm,
-    out_hbm, norms_ref,
+    out_v, norms_ref,
     gate_v, cand_v, weight_v, rates_v, init_v,
     spread, keep_v, base_v, state_v, a_v, b_v, before_a, before_b, whole_a, whole_b,
     diag_v, entry_v, delta_v, low_v, first_low, mixed_v,
     sent1, got1, sent2, got2, start_v, sent3, got3, final_v,
-    load_sem, weight_sem, send1, recv1, send2, recv2, send3, recv3, out_sem,
+    load_sem, weight_sem, send1, recv1, send2, recv2, send3, recv3,
 ):
     f32 = jnp.float32
     place = lax.axis_index("tm")
@@ -41,12 +42,34 @@
     def at(index):
         return (index, part)
 
+    x, z, y = lax.rem(place, NX), lax.rem(place // NX, NZ), place // (NX * NZ)
+    low_z, high_z = lax.rem(z, 2), z // 2
+    xs = [lax.rem(x + d, NX) for d in range(NX)]
+    zs = [lax.rem(z + d, NZ) * NX for d in range(NZ)]
+    ys = [lax.rem(y + d, NY) * (NZ * NX) for d in range(NY)]
+    pair = (z - low_z) * NX + (1 - low_z) * NX
+    beside = [ys[0] + pair + xs[d] for d in (2, 1, 3)]
+    beside += [ys[0] + zs[0] + xs[2], ys[0] + pair + x, ys[0] + zs[0] + xs[1], ys[0] + zs[0] + xs[3]]
+    across = [ys[dy] + lax.rem(z - low_z + dz, NZ) * NX + x for dy in range(NY) for dz in range(2, NZ)]
+    across += [ys[dy] + at_z + x for dy in range(1, NY) for at_z in (zs[0], pair)]
+    everyone = [
+        ys[dy] + zs[dz] + xs[dx]
+        for dz in (4, 3, 5, 2, 6, 1, 7, 0) for dy in (2, 1, 3, 0) for dx in (2, 1, 3, 0)
+        if dy > 0 or dz > 0 or dx > 0
+    ]
+    side = jnp.where(low_z == 1, 1, NZ // 2 - 1)
+    routes = []
+    for dy in range(NY):
+        for hops, dz, flip in ((3, NZ // 4, True), (2, side, False), (1, side, True), (0, 0, False)):
+            if dy == 0 and hops == 0:
+                continue
+            to_z = lax.rem(high_z + dz, NZ // 2) * 2 + (1 - low_z if flip else low_z)
+            other = ys[dy] + to_z * NX + x
+            routes.append((min(dy, NY - dy) + hops, other))
+    routes = [other for _, other in sorted(routes, key=lambda r: -r[0])]
+
     barrier = pltpu.get_barrier_semaphore()
-    for d in range(1, MEMBERS):
-        other = group * MEMBERS + lax.rem(member + d, MEMBERS)
-        pl.semaphore_signal(barrier, inc=1, device_id=at(other), device_id_type=MESH)
-    for d in range(1, groups):
-        other = lax.rem(group + d, groups) * MEMBERS + member
+    for other in beside + across:
         pl.semaphore_signal(barrier, inc=1, device_id=at(other), device_id_type=MESH)
 
     loads = [
@@ -150,9 +173,8 @@
                 sent1[k, pl.ds(first + i * half, half), :] = value
                 got1[k, member, pl.ds(first + i * half, half), :] = value
         if k == 0:
-            pl.semaphore_wait(barrier, MEMBERS - 1 + groups - 1)
-        for d in range(1, MEMBERS):
-            other = group * MEMBERS + lax.rem(member + d, MEMBERS)
+            pl.semaphore_wait(barrier, len(beside) + len(across))
+        for other in beside:
             pltpu.make_async_remote_copy(
                 sent1.at[k], got1.at[k, member], send1.at[k], recv1.at[k],
                 device_id=at(other), device_id_type=MESH,
@@ -168,12 +190,12 @@
             run = joined(run, (got1[k, m, part_a, :], got1[k, m, part_b, :]))
         sent2[k, part_a, :] = run[0]
         sent2[k, part_b, :] = run[1]
-        for d in range(groups - 1, 0, -1):
-            @pl.when(group + d < groups)
+        for i, other in enumerate(routes):
+            @pl.when(other // MEMBERS > group)
             def _():
                 pltpu.make_async_remote_copy(
-                    sent2.at[k], got2.at[k, group], send2.at[k, d], recv2.at[k, group],
-                    device_id=at((group + d) * MEMBERS + member), device_id_type=MESH,
+                    sent2.at[k], got2.at[k, group], send2.at[k, i], recv2.at[k, group],
+                    device_id=at(other), device_id_type=MESH,
                 ).start()
         start_v[...] = jnp.zeros((tiles, LANES), f32)
         for q in range(groups - 1):
@@ -200,15 +222,13 @@
             if k < ITERS - 1:
                 state_v[l, rows, :] = new
             else:
-                spread[0, l, pl.ds(j, BLOCKS, stride=STEPS), :] = new
+                out_v[l, pl.ds(j, BLOCKS, stride=STEPS), :] = new
         if k < ITERS - 1:
             head = jnp.broadcast_to(entry_v[pl.ds(l, 1), :], (BLOCKS, LANES))
             prevs = [jnp.where(block == 0, head, pltpu.roll(states[-1], 1, 0))] + states[:-1]
             for i in range(STEPS // 2):
                 pair = jnp.concatenate(prevs[2 * i : 2 * i + 2], axis=0)
                 low_v[pl.ds(i * 16, 16), cols] = pair.astype(jnp.bfloat16)
-        else:
-            pltpu.make_async_copy(spread.at[0, l], out_hbm.at[:, cols], out_sem.at[l]).start()
         return change
 
     lane = lax.broadcasted_iota(jnp.int32, (1, LANES), 1)
@@ -232,27 +252,33 @@
     sent3[...] = totals
     got3[place] = totals
 
-    def send_total(d, carry):
+    for other in everyone:
         pltpu.make_async_remote_copy(
-            sent3, got3.at[place], send3, recv3,
-            device_id=at(lax.rem(place + d, devices)), device_id_type=MESH,
+            sent3, got3.at[place], send3, recv3, device_id=at(other), device_id_type=MESH
         ).start()
-        return carry
-
-    lax.fori_loop(1, devices, send_total, 0)
     most = got3.at[pl.ds(0, devices - 1)]
-    for l in range(tiles):
-        pltpu.make_async_copy(spread.at[0, l], out_hbm.at[:, pl.ds(l * LANES, LANES)], out_sem.at[l]).wait()
     for k in range(ITERS):
         sent = got1.at[k, pl.ds(0, MEMBERS - 1)]
         pltpu.make_async_copy(sent, sent, send1.at[k]).wait()
-        for d in range(1, groups):
-            @pl.when(group + d < groups)
+        for i, other in enumerate(routes):
+            @pl.when(other // MEMBERS > group)
             def _():
-                pltpu.make_async_copy(sent2.at[k], sent2.at[k], send2.at[k, d]).wait()
+                pltpu.make_async_copy(sent2.at[k], sent2.at[k], send2.at[k, i]).wait()
     pltpu.make_async_copy(most, most, recv3).wait()
     pltpu.make_async_copy(most, most, send3).wait()
     norms_ref[...] = jnp.sqrt(jnp.sum(got3[...], axis=0) * scale)
+
+
+def write(panels, norms, out_hbm, norms_out, sem):
+    copies = [
+        pltpu.make_async_copy(panels.at[l], out_hbm.at[:, pl.ds(l * LANES, LANES)], sem.at[l])
+        for l in range(panels.shape[0])
+    ]
+    for copy in copies:
+        copy.start()
+    norms_out[...] = norms[0, 0:ITERS]
+    for copy in copies:
+        copy.wait()
 
 
 def body(gate_in, cand_in, rates, init_state, recur_weight):
@@ -261,19 +287,22 @@
     groups, tiles = devices // MEMBERS, width // LANES
     f32, bf16 = jnp.float32, jnp.bfloat16
     hbm = pl.BlockSpec(memory_space=pltpu.HBM)
+    vmem = pl.BlockSpec(memory_space=pltpu.VMEM)
     dma = pltpu.SemaphoreType.DMA
     panel = pltpu.VMEM((tiles, rows, LANES), f32)
     edge = pltpu.VMEM((tiles, BLOCKS, LANES), f32)
     ends = pltpu.VMEM((tiles * BLOCKS, LANES), f32)
     units = pltpu.VMEM((tiles, LANES), f32)
+    operands = (gate_in, cand_in, rates.reshape(tiles, LANES), init_state.reshape(tiles, LANES), recur_weight)
+    operands = [pltpu.with_memory_space_constraint(v, pltpu.HBM) for v in operands]
     out, norms = pl.pallas_call(
         functools.partial(kernel, groups, tiles, 1.0 / (rows * devices * width)),
         out_shape=(
-            jax.ShapeDtypeStruct((rows, width), f32),
+            jax.ShapeDtypeStruct((tiles, rows, LANES), f32),
             jax.ShapeDtypeStruct((1, LANES), f32),
         ),
         in_specs=[hbm] * 5,
-        out_specs=(hbm, pl.BlockSpec(memory_space=pltpu.VMEM)),
+        out_specs=(vmem, vmem),
         scratch_shapes=[
             pltpu.VMEM((rows, width), bf16),
             pltpu.VMEM((rows, width), bf16),
@@ -296,12 +325,25 @@
             dma((4,)), dma((8,)),
             dma((ITERS,)), dma((ITERS,)),
             dma((ITERS, groups)), dma((ITERS, groups)),
-            dma, dma, dma((tiles,)),
+            dma, dma,
         ],
-        compiler_params=pltpu.CompilerParams(collective_id=0, has_side_effects=True),
+        compiler_params=pltpu.CompilerParams(
+            collective_id=0, has_side_effects=True, vmem_limit_bytes=32 * 1024 * 1024
+        ),
         name="newton",
-    )(gate_in, cand_in, rates.reshape(tiles, LANES), init_state.reshape(tiles, LANES), recur_weight)
-    return out, norms[0, :ITERS]
+    )(*operands)
+    return pl.pallas_call(
+        write,
+        out_shape=(
+            jax.ShapeDtypeStruct((rows, width), f32),
+            jax.ShapeDtypeStruct((ITERS,), f32),
+        ),
+        in_specs=[vmem, vmem],
+        out_specs=(hbm, vmem),
+        scratch_shapes=[dma((tiles,))],
+        compiler_params=pltpu.CompilerParams(vmem_limit_bytes=4 * 1024 * 1024),
+        name="write",
+    )(out, norms)
 
 
 def solution(mesh):

time: 65.1 us -> 57.3 us (0.88)
  Pallas kernels: 61.1 us -> 56.5 us
  local copies, waits for them, and re-layouts: 2.98 us -> 0 us
    pallas_call x1, Pallas kernels: 61.1 us -> 55 us  [body(): pl.pallas_call(functools.partial(kernel, groups, tiles, 1.0 / (rows * dev...]
    unnamed x1 -> x0, local copies, waits for them, and re-layouts: 1.87 us -> none
    pallas_call x0 -> x1, Pallas kernels: none -> 1.43 us  [body(): pl.pallas_call(write, out_shape=(jax.ShapeDtypeStruct((rows, width), f32)...]
    squeeze x1 -> x0, local copies, waits for them, and re-layouts: 1.11 us -> none  [body(): return (out, norms[0, :ITERS])]
where the time goes in v2:
time: 57.3 us; the launch traced here: 57.1 us
  Pallas kernels  56.5 us (99%)
  between operations  0.64 us (1%)
    pallas_call x1, Pallas kernels, body(): pl.pallas_call(functools.partial(kernel, groups, tiles, 1.0 / (rows * dev...  55 us
    pallas_call x1, Pallas kernels, body(): pl.pallas_call(write, out_shape=(jax.ShapeDtypeStruct((rows, width), f32)...  1.43 us

profile of v2, /device:TPU:8, one launch (start us, length us, event | category | flops | bytes accessed | tf_op | source)
XLA Modules:
  0.0 57.1 jit_solution(13932702058455258063)
XLA Ops:
  0.6 55.0 %newton.1 = (f32[16,64,128]{2,1,0:T(8,128)S(1)}, f32[1,128]{1,0:T(1,128)S(1)}) custom-call(bf16[64,2048]{1,0:T(8,128)(2,1)} %gate_hbm.1, bf16[64,2048]{1,0:T(8,128)(2,1)} %cand_hbm.1, f32[16,128]{1,0:T(8,128)} %bitcast.2, f32[16,128]{1,0:T(8,128)} %bitcast.3, bf16[2048,2048]{1,0:T(8,128)(2,1)} %weight_hbm.1), custom_call_target="tpu_custom_call" | custom-call | tf_op jit(solution)/shard_map/newton/pallas_call | solution.py:298
  55.7 1.4 %write.1 = (f32[64,2048]{1,0:T(8,128)}, f32[3]{0:T(128)}) custom-call(f32[16,64,128]{2,1,0:T(8,128)S(1)} %get-tuple-element.4.panels, f32[1,128]{1,0:T(1,128)S(1)} %get-tuple-element.5.norms), custom_call_target="tpu_custom_call" | custom-call | tf_op jit(solution)/shard_map/write/pallas_call | solution.py:335

commit v3 on v2

--- a/solution.py
+++ b/solution.py
@@ -28,14 +28,13 @@
     gate_v, cand_v, weight_v, rates_v, init_v,
     spread, keep_v, base_v, state_v, a_v, b_v, before_a, before_b, whole_a, whole_b,
     diag_v, entry_v, delta_v, low_v, first_low, mixed_v,
-    sent1, got1, sent2, got2, start_v, sent3, got3, final_v,
-    load_sem, weight_sem, send1, recv1, send2, recv2, send3, recv3,
+    sent1, got1, sent2, got2, start_v, quad_v, got3, sent4, got4, sent5, got5,
+    load_sem, weight_sem, send1, recv1, send2, recv2, send3, recv3, send4, recv4, send5, recv5,
 ):
     f32 = jnp.float32
     place = lax.axis_index("tm")
     part = lax.axis_index("batch")
     group, member = place // MEMBERS, lax.rem(place, MEMBERS)
-    devices = groups * MEMBERS
     width = tiles * LANES
     depth = width // 8
 
@@ -52,11 +51,13 @@
     beside += [ys[0] + zs[0] + xs[2], ys[0] + pair + x, ys[0] + zs[0] + xs[1], ys[0] + zs[0] + xs[3]]
     across = [ys[dy] + lax.rem(z - low_z + dz, NZ) * NX + x for dy in range(NY) for dz in range(2, NZ)]
     across += [ys[dy] + at_z + x for dy in range(1, NY) for at_z in (zs[0], pair)]
-    everyone = [
-        ys[dy] + zs[dz] + xs[dx]
-        for dz in (4, 3, 5, 2, 6, 1, 7, 0) for dy in (2, 1, 3, 0) for dx in (2, 1, 3, 0)
-        if dy > 0 or dz > 0 or dx > 0
+    alike = [
+        ys[dy] + zs[dz] + x
+        for dz in (4, 2, 6, 0) for dy in (2, 1, 3, 0)
+        if dy > 0 or dz > 0
     ]
+    own = tiles // MEMBERS
+    lane = lax.broadcasted_iota(jnp.int32, (1, LANES), 1)
     side = jnp.where(low_z == 1, 1, NZ // 2 - 1)
     routes = []
     for dy in range(NY):
@@ -165,6 +166,73 @@
 
     half = tiles // 2
 
+    def send_squares():
+        constant = jnp.zeros((BLOCKS, LANES), f32)
+        for l in range(tiles):
+            owner, row = l // own, l % own
+            line = jnp.zeros((BLOCKS, LANES), f32)
+            square = jnp.zeros((BLOCKS, LANES), f32)
+            for j in range(STEPS):
+                rows = pl.ds(j * BLOCKS, BLOCKS)
+                a = a_v[l, rows, :]
+                u, v = b_v[l, rows, :] + a * before_b[l], a * before_a[l]
+                constant, line, square = constant + u * u, line + u * v, square + v * v
+            last = pl.ds(l * BLOCKS + BLOCKS - 1, 1)
+            quad_v[owner, pl.ds(row, 1), :] = whole_a[last, :]
+            quad_v[owner, pl.ds(own + row, 1), :] = whole_b[last, :]
+            quad_v[owner, pl.ds(2 * own + row, 1), :] = jnp.sum(line, axis=0, keepdims=True)
+            quad_v[owner, pl.ds(3 * own + row, 1), :] = jnp.sum(square, axis=0, keepdims=True)
+        sent4[4 * own] = jnp.sum(constant, axis=0, keepdims=True)
+        got3[member] = quad_v[member]
+        for other in beside:
+            pltpu.make_async_remote_copy(
+                quad_v.at[lax.rem(other, MEMBERS)], got3.at[member], send3, recv3,
+                device_id=at(other), device_id_type=MESH,
+            ).start()
+
+    def join_squares():
+        most = got3.at[pl.ds(0, MEMBERS - 1)]
+        pltpu.make_async_copy(most, most, recv3).wait()
+        for row in range(own):
+            pa, pb = jnp.ones((1, LANES), f32), jnp.zeros((1, LANES), f32)
+            constant = line = square = jnp.zeros((1, LANES), f32)
+            for m in range(MEMBERS):
+                a, b, q, r = (got3[m, pl.ds(i * own + row, 1), :] for i in range(4))
+                constant = constant + (2.0 * q + r * pb) * pb
+                line = line + (q + r * pb) * pa
+                square = square + r * pa * pa
+                pa, pb = a * pa, a * pb + b
+            for i, value in enumerate((pa, pb, line, square)):
+                sent4[i * own + row] = value
+            sent4[4 * own] = sent4[4 * own] + constant
+        got4[group] = sent4[...]
+        for other in alike:
+            pltpu.make_async_remote_copy(
+                sent4, got4.at[group], send4, recv4, device_id=at(other), device_id_type=MESH
+            ).start()
+
+    def sum_squares():
+        most = got4.at[pl.ds(0, groups - 1)]
+        pltpu.make_async_copy(most, most, recv4).wait()
+        change = jnp.zeros((1, LANES), f32)
+        found = jnp.zeros((1, LANES), f32)
+        for row in range(own):
+            delta = jnp.zeros((1, LANES), f32)
+            for g in range(groups):
+                a, b, q, r = (got4[g, i * own + row] for i in range(4))
+                change = change + (2.0 * q + r * delta) * delta
+                delta = a * delta + b
+        for g in range(groups):
+            change = change + got4[g, 4 * own]
+            found = found + got4[g, 4 * own + 1]
+        found = jnp.where(lane == ITERS - 1, jnp.sum(change), found)
+        sent5[...] = found
+        got5[member] = found
+        for other in beside:
+            pltpu.make_async_remote_copy(
+                sent5, got5.at[member], send5, recv5, device_id=at(other), device_id_type=MESH
+            ).start()
+
     def exchange(k):
         for i in range(2):
             pick = pl.ds(i * half * BLOCKS + BLOCKS - 1, half, stride=BLOCKS)
@@ -179,6 +247,8 @@
                 sent1.at[k], got1.at[k, member], send1.at[k], recv1.at[k],
                 device_id=at(other), device_id_type=MESH,
             ).start()
+        if k == ITERS - 1:
+            send_squares()
         most = got1.at[k, pl.ds(0, MEMBERS - 1)]
         pltpu.make_async_copy(most, most, recv1.at[k]).wait()
 
@@ -197,6 +267,8 @@
                     sent2.at[k], got2.at[k, group], send2.at[k, i], recv2.at[k, group],
                     device_id=at(other), device_id_type=MESH,
                 ).start()
+        if k == ITERS - 1:
+            join_squares()
         start_v[...] = jnp.zeros((tiles, LANES), f32)
         for q in range(groups - 1):
             @pl.when(q < group)
@@ -216,7 +288,8 @@
         for j in range(STEPS):
             rows = pl.ds(j * BLOCKS, BLOCKS)
             moved = b_v[l, rows, :] + a_v[l, rows, :] * carry
-            change = change + moved * moved
+            if k < ITERS - 1:
+                change = change + moved * moved
             new = moved if k == 0 else state_v[l, rows, :] + moved
             states.append(new)
             if k < ITERS - 1:
@@ -231,7 +304,6 @@
                 low_v[pl.ds(i * 16, 16), cols] = pair.astype(jnp.bfloat16)
         return change
 
-    lane = lax.broadcasted_iota(jnp.int32, (1, LANES), 1)
     totals = jnp.zeros((1, LANES), f32)
     for l in range(tiles):
         local_scan(0, l)
@@ -240,8 +312,9 @@
         change = jnp.zeros((BLOCKS, LANES), f32)
         for l in range(tiles):
             change = change + advance(k, l)
-        totals = jnp.where(lane == k, jnp.sum(change), totals)
         if k < ITERS - 1:
+            totals = jnp.where(lane == k, jnp.sum(change), totals)
+            sent4[4 * own + 1] = totals
             wide = 512
             for n in range(width // wide):
                 cols = pl.ds(n * wide, wide)
@@ -249,14 +322,7 @@
                 for l in range(n * wide // LANES, (n + 1) * wide // LANES):
                     local_scan(k + 1, l)
 
-    sent3[...] = totals
-    got3[place] = totals
-
-    for other in everyone:
-        pltpu.make_async_remote_copy(
-            sent3, got3.at[place], send3, recv3, device_id=at(other), device_id_type=MESH
-        ).start()
-    most = got3.at[pl.ds(0, devices - 1)]
+    sum_squares()
     for k in range(ITERS):
         sent = got1.at[k, pl.ds(0, MEMBERS - 1)]
         pltpu.make_async_copy(sent, sent, send1.at[k]).wait()
@@ -264,9 +330,12 @@
             @pl.when(other // MEMBERS > group)
             def _():
                 pltpu.make_async_copy(sent2.at[k], sent2.at[k], send2.at[k, i]).wait()
-    pltpu.make_async_copy(most, most, recv3).wait()
-    pltpu.make_async_copy(most, most, send3).wait()
-    norms_ref[...] = jnp.sqrt(jnp.sum(got3[...], axis=0) * scale)
+    pltpu.make_async_copy(got3.at[pl.ds(0, MEMBERS - 1)], got3.at[pl.ds(0, MEMBERS - 1)], send3).wait()
+    pltpu.make_async_copy(got4.at[pl.ds(0, groups - 1)], got4.at[pl.ds(0, groups - 1)], send4).wait()
+    most = got5.at[pl.ds(0, MEMBERS - 1)]
+    pltpu.make_async_copy(most, most, send5).wait()
+    pltpu.make_async_copy(most, most, recv5).wait()
+    norms_ref[...] = jnp.sqrt(jnp.sum(got5[...], axis=0) * scale)
 
 
 def write(panels, norms, out_hbm, norms_out, sem):
@@ -319,13 +388,16 @@
             pltpu.VMEM((ITERS, 2 * tiles, LANES), f32),
             pltpu.VMEM((ITERS, groups, 2 * tiles, LANES), f32),
             units,
+            pltpu.VMEM((MEMBERS, 4 * tiles // MEMBERS, LANES), f32),
+            pltpu.VMEM((MEMBERS, 4 * tiles // MEMBERS, LANES), f32),
+            pltpu.VMEM((4 * tiles // MEMBERS + 2, 1, LANES), f32),
+            pltpu.VMEM((groups, 4 * tiles // MEMBERS + 2, 1, LANES), f32),
             pltpu.VMEM((1, LANES), f32),
-            pltpu.VMEM((devices, 1, LANES), f32),
-            pltpu.VMEM((8, LANES), f32),
+            pltpu.VMEM((MEMBERS, 1, LANES), f32),
             dma((4,)), dma((8,)),
             dma((ITERS,)), dma((ITERS,)),
             dma((ITERS, groups)), dma((ITERS, groups)),
-            dma, dma,
+            dma, dma, dma, dma, dma, dma,
         ],
         compiler_params=pltpu.CompilerParams(
             collective_id=0, has_side_effects=True, vmem_limit_bytes=32 * 1024 * 1024

time: 57.3 us -> 55.9 us (0.976)
  Pallas kernels: 56.5 us -> 55.1 us
    pallas_call x1, Pallas kernels: 55 us -> 53.7 us  [body(): pl.pallas_call(functools.partial(kernel, groups, tiles, 1.0 / (rows * dev...]
where the time goes in v3:
time: 55.9 us; the launch traced here: 55.8 us
  Pallas kernels  55.1 us (99%)
  between operations  0.64 us (1%)
    pallas_call x1, Pallas kernels, body(): pl.pallas_call(functools.partial(kernel, groups, tiles, 1.0 / (rows * dev...  53.7 us
    pallas_call x1, Pallas kernels, body(): pl.pallas_call(write, out_shape=(jax.ShapeDtypeStruct((rows, width), f32)...  1.43 us

profile of v3, /device:TPU:8, one launch (start us, length us, event | category | flops | bytes accessed | tf_op | source)
XLA Modules:
  0.0 55.8 jit_solution(15795394383760222520)
XLA Ops:
  0.6 53.7 %newton.1 = (f32[16,64,128]{2,1,0:T(8,128)S(1)}, f32[1,128]{1,0:T(1,128)S(1)}) custom-call(bf16[64,2048]{1,0:T(8,128)(2,1)} %gate_hbm.1, bf16[64,2048]{1,0:T(8,128)(2,1)} %cand_hbm.1, f32[16,128]{1,0:T(8,128)} %bitcast.2, f32[16,128]{1,0:T(8,128)} %bitcast.3, bf16[2048,2048]{1,0:T(8,128)(2,1)} %weight_hbm.1), custom_call_target="tpu_custom_call" | custom-call | tf_op jit(solution)/shard_map/newton/pallas_call | solution.py:367
  54.3 1.4 %write.1 = (f32[64,2048]{1,0:T(8,128)}, f32[3]{0:T(128)}) custom-call(f32[16,64,128]{2,1,0:T(8,128)S(1)} %get-tuple-element.4.panels, f32[1,128]{1,0:T(1,128)S(1)} %get-tuple-element.5.norms), custom_call_target="tpu_custom_call" | custom-call | tf_op jit(solution)/shard_map/write/pallas_call | solution.py:407
